TPU v7x, 32 devices: a whole 2x2x4 slice. The times are simulated.
32 devices in a mesh: grp: 2 (over x), slab: 16 (over z, y, core).
Axes of the slice: x: 2, y: 2, z: 4, core: 2. Of those that a mesh axis runs over, the one named last changes fastest.
Arguments:
- volume: bfloat16 [64, 1024, 1024], P(('grp', 'slab')), parts along dimension 0, may hold values from -60 to 60
- plane_shift: int32 [4, 32], P('grp', 'slab'), parts along dimension 0, may hold values from -64 to 64
- plane_weight: float32 [4, 32], P('grp', 'slab'), parts along dimension 0, may hold values from 0 to 1
- column_left: int32 [4, 1024], P('grp'), parts along dimension 0, may hold values from 0 to 1022
- column_weight: float32 [4, 1024], P('grp'), parts along dimension 0, may hold values from 0 to 1
- window_center: int32 [4, 2], P('grp'), parts along dimension 0, may hold values from -200 to 199
- tilt_owner: int32 [32], P('grp'), parts along dimension 0, may hold values from 0 to 15, each once
- reference_band: float32 [32, 2, 128, 128], P(('grp', 'slab')), parts along dimension 0, may hold values from -6 to 6
Outputs:
- correlation: float32 [4, 16, 128], P('grp', 'slab'), parts along dimension 0
- peaks: float32 [4], P('grp'), parts along dimension 0
There are 2 independent parts, one for each index of `grp`. A program takes and returns all parts, laid end to end along the dimension named above; each array names one. Nothing has to cross between parts.
Inputs may be any that keep to these rules, and one draw needn't show every extreme that they name: `tilt_owner`: the first 2 entries name the owners of the tilts, one slab index each.
All inputs are finite; a program needn't handle non-finite values.
Results may differ from a plain program's by a relative error of at most 0.0003.
Values sent between devices are 32-bit elements; how exact they have to be, the bound alone decides.
A program may use at most 128 MiB of HBM per device.

v0:
```python
import math

import jax
import jax.numpy as jnp
from jax import lax
from jax.sharding import PartitionSpec as P

Y = 1024
X = 1024
BAND = 128
WIN_COLS = 128
TILTS = 2
WIN_ROWS_DEV = 1


def from_root(value, axis, source):
    kept = jnp.where(lax.axis_index(axis) == source, value, 0).astype(value.dtype)
    return lax.psum(kept, axis)


def phase_pair(left_ints, right_ints, length):
    product = left_ints[:, None] * right_ints[None, :] % length
    angle = product.astype(jnp.float32) * (2.0 * math.pi / length)
    return (jnp.cos(angle), jnp.sin(angle))


def matmul(first, second):
    return jnp.dot(
        first, second, precision=lax.Precision.HIGHEST, preferred_element_type=jnp.float32
    )


def reproject(volume, shifts, weights, left_cols, right_share, row_count):
    grid_width = volume.shape[2]
    margin = grid_width // 16 + 1
    padded_all = jnp.pad(volume, ((0, 0), (0, 0), (margin, margin)))
    summed = jnp.zeros((row_count, grid_width), jnp.float32)
    for plane_no in range(volume.shape[0]):
        padded = padded_all[plane_no]
        near_cells = lax.dynamic_slice_in_dim(
            padded, margin - shifts[plane_no], grid_width, 1
        ).astype(jnp.float32)
        far_cells = lax.dynamic_slice_in_dim(
            padded, margin - shifts[plane_no] - 1, grid_width, 1
        ).astype(jnp.float32)
        summed = summed + (1.0 - weights[plane_no]) * near_cells + weights[plane_no] * far_cells
    left_values = jnp.take(summed, left_cols, axis=1)
    right_values = jnp.take(summed, left_cols + 1, axis=1)
    return (1.0 - right_share) * left_values + right_share * right_values


def band_part(projected):
    row_count, grid_width = projected.shape
    freq_cols = jnp.arange(BAND, dtype=jnp.int32)
    freq_rows = freq_cols - BAND // 2
    col_cos, col_sin = phase_pair(jnp.arange(grid_width, dtype=jnp.int32), freq_cols, grid_width)
    real_half = matmul(projected, col_cos)
    imag_half = -matmul(projected, col_sin)
    row_ids = jnp.arange(row_count, dtype=jnp.int32)
    row_cos, row_sin = phase_pair(freq_rows, row_ids, Y)
    spec_real = matmul(row_cos, real_half) + matmul(row_sin, imag_half)
    spec_imag = matmul(row_cos, imag_half) - matmul(row_sin, real_half)
    return jnp.stack([spec_real, spec_imag])


def correlate(spectrum, owned, center, row_ids, total_rows):
    spec_real, spec_imag = (spectrum[0], spectrum[1])
    ref_real, ref_imag = (owned[0], owned[1])
    cross_real = spec_real * ref_real + spec_imag * ref_imag
    cross_imag = spec_imag * ref_real - spec_real * ref_imag
    energy_spec = jnp.mean(spec_real * spec_real + spec_imag * spec_imag) + 1e-06
    energy_ref = jnp.mean(ref_real * ref_real + ref_imag * ref_imag) + 1e-06
    freq_cols = jnp.arange(BAND, dtype=jnp.int32)
    freq_rows = freq_cols - BAND // 2
    offsets_y = center[0] + row_ids - total_rows // 2
    offsets_x = center[1] + jnp.arange(WIN_COLS, dtype=jnp.int32) - WIN_COLS // 2
    row_cos, row_sin = phase_pair(offsets_y, freq_rows, Y)
    col_cos, col_sin = phase_pair(freq_cols, offsets_x, X)
    half_real = matmul(row_cos, cross_real) - matmul(row_sin, cross_imag)
    half_imag = matmul(row_cos, cross_imag) + matmul(row_sin, cross_real)
    return (matmul(half_real, col_cos) - matmul(half_imag, col_sin)) / (
        BAND * jnp.sqrt(energy_spec * energy_ref)
    )


def per_device(
    volume,
    plane_shift,
    plane_weight,
    column_left,
    column_weight,
    window_center,
    tilt_owner,
    reference_band,
):
    devices = lax.axis_size("slab")
    position = lax.axis_index("slab")
    partials = []
    for which in range(TILTS):

        def rows_term(first_row, row_count, which=which):
            return reproject(
                volume,
                plane_shift[which],
                plane_weight[which],
                column_left[which],
                column_weight[which],
                row_count,
            )

        partials.append(band_part(rows_term(0, Y)))
    stacked = jnp.stack(partials)
    mine = reference_band[0]
    spectra = lax.psum(stacked, "slab")
    references = jnp.stack([from_root(mine, "slab", tilt_owner[which]) for which in range(TILTS)])
    total_rows = WIN_ROWS_DEV * devices
    outputs = []
    maxima = []
    row_ids = position * WIN_ROWS_DEV + jnp.arange(WIN_ROWS_DEV, dtype=jnp.int32)
    for which in range(TILTS):
        corr = correlate(
            spectra[which], references[which], window_center[which], row_ids, total_rows
        )
        outputs.append(corr)
        maxima.append(jnp.max(corr))
    peaks = lax.pmax(jnp.stack(maxima), "slab")
    return (jnp.stack(outputs), peaks)


def solution(mesh):
    placed = (
        P(("grp", "slab"), None, None),
        P("grp", "slab"),
        P("grp", "slab"),
        P("grp", None),
        P("grp", None),
        P("grp", None),
        P("grp"),
        P(("grp", "slab"), None, None, None),
    )
    return jax.shard_map(
        per_device,
        mesh=mesh,
        in_specs=placed,
        out_specs=(P("grp", "slab", None), P("grp")),
        check_vma=False,
    )
```

profile of v0, /device:TPU:0, one launch (start us, length us, event | category | flops | bytes accessed | tf_op | source)
XLA Modules:
  0.0 311.5 jit_solution(11527147601551082680)
XLA Ops:
  7.2 0.0 all-reduce.4.cloned.1.call-start
  7.2 1.4 fusion.201
  19.0 0.8 fusion.198
  19.9 1.5 fusion.200
  24.0 6.2 %copy.10 = bf16[2,1024,1024]{1,2,0:T(8,128)(2,1)} copy(bf16[2,1024,1024]{2,1,0:T(8,128)(2,1)} %param.10) | data formatting | bytes 8388608 | tf_op args[0]
  30.2 5.0 %pad_slice_fusion.1 = (bf16[1,1024,1154]{1,2,0:T(8,128)(2,1)S(1)}, bf16[1,1024,1154]{1,2,0:T(8,128)(2,1)}) fusion(bf16[2,1024,1024]{1,2,0:T(8,128)(2,1)} %copy.10), kind=kLoop, calls=%fused_computation.5 | loop fusion | bytes 8921088 | tf_op jit(solution)/shard_map/slice | solution.py:39
  35.2 12.7 %add_bitcast_fusion.1 = (f32[1024,1024]{0,1:T(8,128)}, f32[1024,1024]{0,1:T(8,128)}) fusion(bf16[1,1024,1154]{1,2,0:T(8,128)(2,1)} %get-tuple-element.11, s32[]{:T(128)S(6)} %select_n.127, f32[]{:T(128)} %bitcast.11, s32[]{:T(128)S(6)} %select_n.126, f32[]{:T(128)S(6)} %sub.140, bf16[1,1024,1154]{1,2,0:T(8,128)(2,1)S(1)} %get-tuple-element.10, ...), kind=kLoop, calls=%fused_computation.13 | loop fusion | flops 23068672 | bytes 25165888 | tf_op jit(solution)/shard_map/add | solution.py:46
  47.8 8.6 %gather_fusion.2 = f32[1024,1024]{1,0:T(8,128)} fusion(f32[1024,1024]{0,1:T(8,128)} %get-tuple-element.9, s32[1024]{0:T(1024)S(1)} %get-tuple-element.34), kind=kCustom, calls=%fused_computation.2.clone | custom fusion | bytes 8392704 | tf_op jit(solution)/shard_map/jit(_take)/gather | solution.py:47
  56.4 0.0 copy-start.1
  56.4 8.6 %gather_fusion.3 = f32[1024,1024]{1,0:T(8,128)} fusion(f32[1024,1024]{0,1:T(8,128)} %get-tuple-element.9, s32[1024]{0:T(1024)S(1)} %get-tuple-element.35), kind=kCustom, calls=%fused_computation.3.clone | custom fusion | bytes 8392704 | tf_op jit(solution)/shard_map/jit(_take)/gather | solution.py:48
  65.0 0.0 copy-done.1
  65.0 4.4 %fusion = f32[1024,1024]{0,1:T(8,128)S(1)} fusion(f32[1024,1024]{1,0:T(8,128)} %gather_fusion.3, f32[1024,1024]{1,0:T(8,128)} %gather_fusion.2, f32[1024]{0:T(1024)S(1)} %bitcast.250, f32[1024]{0:T(1024)S(1)} %bitcast.249, pred[1024]{0:T(1024)(128)(4,1)S(1)} %get-tuple-element.33, pred[1024]{0:T(1024)(128)(4,1)S(1)} %get-tuple-element.32), kind=kLoop, calls=%fused_computation.7 | loop fusion | flops 5242880 | bytes 12593152 | tf_op jit(solution)/shard_map/add | solution.py:49
  69.4 8.5 %fusion.32 = f32[1024,128]{1,0:T(8,128)S(1)} fusion(f32[1024,1024]{0,1:T(8,128)S(1)} %fusion), kind=kOutput, calls=%fused_computation.69 | convolution fusion | flops 1612447744 | bytes 4718592 | tf_op jit(solution)/shard_map/dot_general | solution.py:28
  77.9 21.3 %convolution_negate_fusion = f32[1024,128]{1,0:T(8,128)S(1)} fusion(f32[1024,1024]{0,1:T(8,128)S(1)} %fusion), kind=kOutput, calls=%fused_computation.14 | convolution fusion | flops 1612578816 | bytes 4718592 | tf_op jit(solution)/shard_map/dot_general | solution.py:28
  99.3 8.6 %gather_fusion = f32[1024,1024]{1,0:T(8,128)} fusion(f32[1024,1024]{0,1:T(8,128)} %get-tuple-element.8, s32[1024]{0:T(1024)S(1)} %get-tuple-element.30), kind=kCustom, calls=%fused_computation.clone | custom fusion | bytes 8392704 | tf_op jit(solution)/shard_map/jit(_take)/gather | solution.py:47
  107.8 8.6 %gather_fusion.1 = f32[1024,1024]{1,0:T(8,128)} fusion(f32[1024,1024]{0,1:T(8,128)} %get-tuple-element.8, s32[1024]{0:T(1024)S(1)} %get-tuple-element.31), kind=kCustom, calls=%fused_computation.1.clone | custom fusion | bytes 8392704 | tf_op jit(solution)/shard_map/jit(_take)/gather | solution.py:48
  116.5 4.0 %fusion.1 = f32[1024,1024]{0,1:T(8,128)S(1)} fusion(f32[1024,1024]{1,0:T(8,128)} %gather_fusion.1, f32[1024,1024]{1,0:T(8,128)} %gather_fusion, f32[1024]{0:T(1024)S(1)} %bitcast.248, f32[1024]{0:T(1024)S(1)} %bitcast.247, pred[1024]{0:T(1024)(128)(4,1)S(1)} %get-tuple-element.29, pred[1024]{0:T(1024)(128)(4,1)S(1)} %get-tuple-element.28), kind=kLoop, calls=%fused_computation.10 | loop fusion | flops 5242880 | bytes 12593152 | tf_op jit(solution)/shard_map/add | solution.py:49
  120.5 8.5 %fusion.34 = f32[1024,128]{1,0:T(8,128)S(1)} fusion(f32[1024,1024]{0,1:T(8,128)S(1)} %fusion.1), kind=kOutput, calls=%fused_computation.70 | convolution fusion | flops 1612447744 | bytes 4718592 | tf_op jit(solution)/shard_map/dot_general | solution.py:28
  129.0 8.9 %convolution_negate_fusion.1 = f32[1024,128]{1,0:T(8,128)S(1)} fusion(f32[1024,1024]{0,1:T(8,128)S(1)} %fusion.1), kind=kOutput, calls=%fused_computation.15 | convolution fusion | flops 1612578816 | bytes 4718592 | tf_op jit(solution)/shard_map/dot_general | solution.py:28
  137.9 3.0 fusion.42
  140.9 3.0 fusion.40
  143.9 3.0 fusion.3
  146.9 3.0 fusion.2
  149.9 0.0 copy-start.3
  149.9 3.0 fusion.46
  152.9 0.0 copy-start
  152.9 0.0 copy-start.2
  152.9 3.2 %fusion.44 = f32[128,128]{1,0:T(8,128)S(1)} fusion(f32[1024,128]{1,0:T(8,128)S(1)} %convolution_negate_fusion.1, s32[128]{0:T(128)S(1)} %iota_add_fusion), kind=kOutput, calls=%fused_computation.75 | convolution fusion | flops 203161600 | bytes 590336 | tf_op jit(solution)/shard_map/dot_general | solution.py:28
  156.1 3.0 fusion.5
  159.1 3.0 fusion.4
  162.1 0.0 copy-done.3
  162.2 0.6 fusion.202
  164.1 0.7 pad_maximum_fusion
  164.8 0.0 copy-done
  164.8 0.7 select_bitcast_fusion.1
  165.5 0.0 all-reduce.4.cloned.1.call-update
  165.5 0.0 copy-done.2
  165.5 0.7 fusion.199
  167.4 0.7 add_add_fusion.1
  168.1 0.6 add_add_fusion
  168.7 90.9 %all-reduce.4.cloned.1.call-done = (f32[2,2,128,128]{3,2,1,0:T(8,128)}, f32[2,128,128]{2,1,0:T(8,128)}, f32[2,128,128]{2,1,0:T(8,128)}) async-done(((f32[2,2,128,128]{3,2,1,0:T(8,128)}, f32[2,128,128]{2,1,0:T(8,128)}, f32[2,128,128]{2,1,0:T(8,128)}), (f32[2,2,128,128]{3,2,1,0:T(8,128)}, f32[2,128,128]{2,1,0:T(8,128)}, f32[2,128,128]{2,1,0:T(8,128)})) %all-reduce.4.cloned.1.call-update) | async-done | bytes 524304 | tf_op jit(solution)/shard_map/psum | solution.py:114
  259.6 1.7 multiply_subtract_fusion.1
  261.4 0.2 convolution_bitcast_fusion.8
  261.6 0.2 convolution_bitcast_fusion.11
  261.8 0.2 fusion.13
  262.0 0.2 fusion.15
  263.6 1.6 multiply_subtract_fusion
  265.2 0.2 convolution_bitcast_fusion.2
  265.4 0.2 convolution_bitcast_fusion.5
  265.6 0.2 fusion.8
  265.8 0.2 fusion.10
  267.4 0.4 convolution_bitcast_fusion.9
  267.8 0.4 convolution_bitcast_fusion.3
  268.2 1.0 fusion.204
  269.2 1.0 fusion.203
  270.2 1.4 pad_maximum_fusion.2
  271.6 32.3 %pmax.7 = f32[2]{0:T(128)} all-reduce(f32[2]{0:T(128)S(1)} %pad_maximum_fusion.2), channel_id=1, replica_groups=mesh['grp'=2,'slab'=16] {'slab'}, use_global_device_ids=true, to_apply=%region_9.11 | all-reduce | flops 2 | bytes 16 | tf_op jit(solution)/shard_map/pmax | solution.py:126
  303.9 0.6 pad_maximum_fusion.1
  (7 shorter events, 0.1 us)
Async XLA Ops:
  7.2 252.5 %all-reduce.4.cloned.1.call-start = ((), (), s32[]{:S(2)}) async-start(), calls=%async_computation | async-start | bytes 1048576 | tf_op jit(solution)/shard_map/psum | solution.py:114
  56.4 8.6 %copy-start.1 = (f32[2,1024]{1,0:T(2,128)S(1)}, f32[2,1024]{1,0:T(2,128)}, u32[]{:S(2)}) copy-start(f32[2,1024]{1,0:T(2,128)} %param.14) | copy-start | bytes 24580
  149.9 12.2 %copy-start.3 = (s32[16]{0:T(128)S(1)}, s32[16]{0:T(128)}, u32[]{:S(2)}) copy-start(s32[16]{0:T(128)} %param.16) | copy-start | bytes 196
  152.9 11.8 %copy-start = (f32[1,2,128,128]{3,2,1,0:T(8,128)S(1)}, f32[1,2,128,128]{3,2,1,0:T(8,128)}, u32[]{:S(2)}) copy-start(f32[1,2,128,128]{3,2,1,0:T(8,128)} %param.17) | copy-start | bytes 393220
  152.9 12.6 %copy-start.2 = (s32[2,2]{1,0:T(2,128)S(1)}, s32[2,2]{1,0:T(2,128)}, u32[]{:S(2)}) copy-start(s32[2,2]{1,0:T(2,128)} %param.15) | copy-start | bytes 52
Sparse Core Ops, SparseCore 0:
  165.6 93.9 all-reduce.3
where the time goes:
time: 317 us; the launch traced here: 311 us
  waiting for transfers between devices  90.9 us (29%)
  matrix products  75.9 us (24%)
  local copies, waits for them, and re-layouts  50.6 us (16%)
  between operations  32.7 us (10%)
  blocking collectives  32.3 us (10%)
  other arithmetic  29 us (9%)
    psum x1, waiting for transfers between devices, per_device(): spectra = lax.psum(stacked, 'slab')  90.9 us
    dot_general x24, matrix products, matmul(): jnp.dot(first, second, precision=lax.Precision.HIGHEST, preferred_element...  75.9 us
    pmax x1, blocking collectives, per_device(): peaks = lax.pmax(jnp.stack(maxima), 'slab')  32.3 us
    gather x2, local copies, waits for them, and re-layouts, reproject(): right_values = jnp.take(summed, left_cols + 1, axis=1)  17.2 us
    gather x2, local copies, waits for them, and re-layouts, reproject(): left_values = jnp.take(summed, left_cols, axis=1)  17.2 us
    add x1, other arithmetic, reproject(): summed + (1.0 - weights[plane_no]) * near_cells  12.7 us
    add x2, other arithmetic, reproject(): return (1.0 - right_share) * left_values + right_share * right_values  8.41 us
  transfers between devices with their start and end apart: 1, of which 1 were waited for; matrix products, arithmetic and copies ran while one was open for 1% of the time, Pallas kernels for 0%

commit v1 on v0

v1 whole, which is shorter than its diff:
```python
import functools
import math

import jax
import jax.numpy as jnp
import numpy as np
from jax import lax
from jax.experimental import pallas as pl
from jax.experimental.pallas import tpu as pltpu
from jax.sharding import PartitionSpec as P

MESH = pl.DeviceIdType.MESH
LANES = 128
CHUNK = 256
BF16 = jnp.bfloat16
F32 = jnp.float32


def phases(left, right, length):
    angle = (np.outer(left, right) % length) * (2.0 * math.pi / length)
    return np.cos(angle), np.sin(angle)


def split(values):
    high = values.astype(np.float32).astype(BF16)
    low = (values - high.astype(np.float64)).astype(np.float32).astype(BF16)
    return high, low


def halves(value):
    high = value.astype(BF16)
    return high, (value - high.astype(F32)).astype(BF16)


def row_table(length, band):
    count = band // 2 + 8
    cos, sin = phases(np.arange(count), np.arange(length), length)
    return np.concatenate(split(np.concatenate([cos, sin])))


def col_table(length, band):
    cos, sin = phases(np.arange(length), np.arange(band), length)
    return np.stack(split(np.concatenate([cos, sin], axis=1)))


def window_table(length, band, columns):
    cos, sin = phases(np.arange(band), np.arange(columns), length)
    return np.concatenate([cos, sin], axis=1).astype(np.float32)


def partial_kernel(
    shift_ref, weight_ref, left_ref, share_ref, volume_ref, rowt_ref, colt_ref, out_ref,
    vol, rowt, colt, onehot, rows, rolled, summed, stack, proj, sems,
):
    planes, height, width = volume_ref.shape
    tilts = left_ref.shape[0]
    blocks = width // LANES
    chunks = width // CHUNK
    count = rows.shape[2]

    table = pltpu.make_async_copy(rowt_ref, rowt, sems.at[0])
    table.start()
    loads = []
    for z in range(planes):
        for c in range(chunks):
            part = (z, slice(None), pl.ds(c * CHUNK, CHUNK))
            load = pltpu.make_async_copy(volume_ref.at[part], vol.at[part], sems.at[2 + z * chunks + c])
            load.start()
            loads.append(load)
    last_table = pltpu.make_async_copy(colt_ref, colt, sems.at[1])
    last_table.start()

    @pl.loop(0, blocks)
    def _(b):
        first = pl.multiple_of(b * LANES, LANES)
        ids = lax.broadcasted_iota(jnp.int32, (LANES, width), 0) + first
        for t in range(tilts):
            hit = jnp.where(ids == left_ref[t : t + 1, :], 1.0, 0.0)
            onehot[t, pl.ds(first, LANES), :] = hit.astype(BF16)

    table.wait()
    for z in range(planes):
        for c in range(chunks):
            loads[z * chunks + c].wait()
            out = jnp.dot(
                rowt[...], vol[z, :, c * CHUNK : (c + 1) * CHUNK], preferred_element_type=F32
            )
            out = out[:count] + out[count:]
            for b in range(CHUNK // LANES):
                rows[z, c * (CHUNK // LANES) + b] = out[:, b * LANES : (b + 1) * LANES]

    lane = lax.broadcasted_iota(jnp.int32, (count, LANES), 1)
    zero = jnp.zeros((count, LANES), F32)
    for t in range(tilts):
        terms = []
        for z in range(planes):
            for extra in range(2):
                slot = z * 2 + extra
                shift = shift_ref[t, z] + extra
                turn = shift & (LANES - 1)
                jump = jnp.where(shift < 0, 1, 0)
                weight = weight_ref[t, z] if extra else 1.0 - weight_ref[t, z]
                rolled[slot, 0] = zero
                rolled[slot, blocks + 1] = zero
                for b in range(blocks):
                    rolled[slot, b + 1] = pltpu.roll(rows[z, b] * weight, turn, 1)
                terms.append((slot, lane >= turn, jump))
        for b in range(blocks):
            total = None
            for slot, mask, jump in terms:
                term = jnp.where(mask, rolled[slot, b + 1 + jump], rolled[slot, b + jump])
                total = term if total is None else total + term
            summed[b] = total
            high, low = halves(total)
            here = slice(b * LANES, (b + 1) * LANES)
            stack[0, :, here] = high
            stack[1, :, here] = low
        for b in range(blocks):
            ahead = summed[(b + 1) % blocks]
            right = pltpu.roll(jnp.where(lane == 0, ahead, summed[b]), LANES - 1, 1)
            high, low = halves(right)
            here = slice(b * LANES, (b + 1) * LANES)
            stack[2, :, here] = high
            stack[3, :, here] = low
        for c in range(chunks):
            here = slice(c * CHUNK, (c + 1) * CHUNK)
            picked = jnp.dot(
                stack[...].reshape(4 * count, width), onehot[t, :, here], preferred_element_type=F32
            )
            share = share_ref[t : t + 1, here]
            value = (1.0 - share) * (picked[:count] + picked[count : 2 * count])
            value = value + share * (picked[2 * count : 3 * count] + picked[3 * count :])
            high, low = halves(value)
            proj[0, :, here] = high
            proj[1, :, here] = low
        if t == 0:
            last_table.wait()
        both = jnp.dot(
            proj[...].reshape(2 * count, width), colt[0], preferred_element_type=F32
        )
        rest = jnp.dot(proj[0], colt[1], preferred_element_type=F32)
        out_ref[t] = both[:count] + both[count:] + rest


def partial_spectra(shift, weight, left, share, volume, band):
    planes, height, width = volume.shape
    tilts = left.shape[0]
    rowt = row_table(height, band)
    colt = col_table(width, band)
    count = rowt.shape[0] // 2
    blocks = width // LANES
    smem = pl.BlockSpec(memory_space=pltpu.SMEM)
    vmem = pl.BlockSpec(memory_space=pltpu.VMEM)
    hbm = pl.BlockSpec(memory_space=pl.ANY)
    return pl.pallas_call(
        partial_kernel,
        out_shape=jax.ShapeDtypeStruct((tilts, count, 2 * band), F32),
        in_specs=[smem, smem, vmem, vmem, hbm, hbm, hbm],
        out_specs=vmem,
        scratch_shapes=[
            pltpu.VMEM((planes, height, width), BF16),
            pltpu.VMEM(rowt.shape, BF16),
            pltpu.VMEM(colt.shape, BF16),
            pltpu.VMEM((tilts, width, width), BF16),
            pltpu.VMEM((planes, blocks, count, LANES), F32),
            pltpu.VMEM((planes * 2, blocks + 2, count, LANES), F32),
            pltpu.VMEM((blocks, count, LANES), F32),
            pltpu.VMEM((4, count, width), BF16),
            pltpu.VMEM((2, count, width), BF16),
            pltpu.SemaphoreType.DMA((2 + planes * (width // CHUNK),)),
        ],
        compiler_params=pltpu.CompilerParams(vmem_limit_bytes=56 * 1024 * 1024),
        name="partial_spectra",
    )(shift, weight, left, share, volume, jnp.asarray(rowt), jnp.asarray(colt))


def exchange_kernel(
    n, length, center_ref, owner_ref, partial_ref, mine_ref, window_ref, corr_ref, peak_ref,
    ref_out, ref_in, spec_out, spec_in, part_out, part_in, total_ref,
    ref_send, ref_recv, spec_send, spec_recv, part_send, part_recv,
):
    me = lax.axis_index("slab")
    tilts, count, _ = partial_ref.shape
    band = mine_ref.shape[-1]
    half = band // 2
    sines = count // 2
    per = max(1, half // n)
    owners = half // per
    win_cols = corr_ref.shape[-1]

    def on_owner(device, body):
        if owners == n:
            body()
        else:
            pl.when(device < owners)(body)

    barrier = pltpu.get_barrier_semaphore()
    for k in range(1, n):
        pl.semaphore_signal(
            barrier, inc=1, device_id={"slab": lax.rem(me + k, n)}, device_id_type=MESH
        )

    for e in range(owners):
        for part in range(2):
            base = part * 2 * per
            first = half + e * per
            ref_out[e, base : base + per, :] = mine_ref[0, part, first : first + per, :]
            for k in range(per):
                row = (half - e * per - k) if e * per + k else 0
                ref_out[e, base + per + k : base + per + k + 1, :] = mine_ref[0, part, row : row + 1, :]

    top = lax.broadcasted_iota(jnp.int32, (half, band), 0) == 0
    for t in range(tilts):
        cos_cos = partial_ref[t, :sines, :band]
        cos_sin = partial_ref[t, :sines, band:]
        sin_cos = partial_ref[t, sines:, :band]
        sin_sin = partial_ref[t, sines:, band:]
        low_re = cos_cos + sin_sin
        low_im = sin_cos - cos_sin
        kinds = (
            (cos_cos - sin_sin)[:half],
            jnp.where(top, low_re[half : half + 1], low_re[:half]),
            -(sin_cos + cos_sin)[:half],
            jnp.where(top, low_im[half : half + 1], low_im[:half]),
        )
        for kind, value in enumerate(kinds):
            base = (t * 4 + kind) * per
            for e in range(owners):
                spec_out[e, base : base + per, :] = value[e * per : (e + 1) * per]

    pl.semaphore_wait(barrier, n - 1)

    def copy_of(out, into, send, recv, k):
        dest = lax.rem(me + k, n)
        return pltpu.make_async_remote_copy(
            src_ref=out.at[dest] if out.shape[0] == owners and len(out.shape) == 3 else out,
            dst_ref=into.at[me],
            send_sem=send.at[k],
            recv_sem=recv.at[k],
            device_id={"slab": dest},
            device_id_type=MESH,
        )

    def waiter(out, into, send, recv, k):
        source = lax.rem(me + n - k, n)
        return pltpu.make_async_remote_copy(
            src_ref=out.at[0] if len(out.shape) == 3 else out,
            dst_ref=into.at[source],
            send_sem=send.at[k],
            recv_sem=recv.at[k],
            device_id={"slab": source},
            device_id_type=MESH,
        )

    scatters = ((spec_out, spec_in, spec_send, spec_recv), (ref_out, ref_in, ref_send, ref_recv))
    for group in scatters:
        for k in range(1, n):
            on_owner(lax.rem(me + k, n), lambda: copy_of(*group, k).start())

    def wave(ints):
        angle = (ints & (length - 1)).astype(F32) * (2.0 * math.pi / length)
        return jnp.cos(angle), jnp.sin(angle)

    freq = lax.broadcasted_iota(jnp.int32, (2 * per, band), 1)
    slot = lax.broadcasted_iota(jnp.int32, (n, 2 * per), 1)
    step = lax.broadcasted_iota(jnp.int32, (n, 2 * per), 0) - n // 2
    lower = slot >= per
    place = me * per + jnp.where(lower, slot - per, slot)
    freq_row = jnp.where(lower, jnp.where(place == 0, -half, -place), place)
    col_waves = [wave(freq * (center_ref[t, 1] - win_cols // 2)) for t in range(tilts)]
    row_waves = [wave(freq_row * (center_ref[t, 0] + step)) for t in range(tilts)]

    def contribute():
        spec_in[me] = spec_out[me]
        ref_in[me] = ref_out[me]
        for group in reversed(scatters):
            for k in range(1, n):
                waiter(*group, k).wait_recv()
        total = spec_in[0]
        for e in range(1, n):
            total = total + spec_in[e]
        real_parts, imag_parts, powers = [], [], []
        ref_powers = []
        for t in range(tilts):
            base = t * 4 * per
            spec_re = total[base : base + 2 * per]
            spec_im = total[base + 2 * per : base + 4 * per]
            owned = ref_in[owner_ref[t]]
            ref_re, ref_im = owned[: 2 * per], owned[2 * per :]
            cross_re = spec_re * ref_re + spec_im * ref_im
            cross_im = spec_im * ref_re - spec_re * ref_im
            cos, sin = col_waves[t]
            real_parts.append(cross_re * cos - cross_im * sin)
            imag_parts.append(cross_re * sin + cross_im * cos)
            powers.append(jnp.sum(spec_re * spec_re + spec_im * spec_im, axis=0, keepdims=True))
            ref_powers.append(jnp.sum(ref_re * ref_re + ref_im * ref_im, axis=0, keepdims=True))
        turned = jnp.dot(
            jnp.concatenate(real_parts + imag_parts, axis=0), window_ref[...],
            precision=lax.Precision.HIGHEST, preferred_element_type=F32,
        )
        mid = tilts * 2 * per
        moved_re = turned[:mid, :win_cols] - turned[mid:, win_cols:]
        moved_im = turned[:mid, win_cols:] + turned[mid:, :win_cols]
        for t in range(tilts):
            here = slice(t * 2 * per, (t + 1) * 2 * per)
            cos, sin = row_waves[t]
            left = jnp.concatenate([cos, -sin], axis=1)
            right = jnp.concatenate([moved_re[here], moved_im[here]], axis=0)
            part_out[t * n : (t + 1) * n, :] = jnp.dot(
                left, right, precision=lax.Precision.HIGHEST, preferred_element_type=F32
            )
            part_out[tilts * n + t : tilts * n + t + 1, :] = powers[t]
            part_out[tilts * n + tilts + t : tilts * n + tilts + t + 1, :] = ref_powers[t]
        for k in range(1, n):
            copy_of(part_out, part_in, part_send, part_recv, k).start()
        part_in[me] = part_out[...]

    part_out[tilts * n :, :] = jnp.zeros_like(part_out[tilts * n :, :])
    on_owner(me, contribute)

    for k in range(1, n):
        source = lax.rem(me + n - k, n)
        on_owner(source, lambda: waiter(part_out, part_in, part_send, part_recv, k).wait_recv())
    total = part_in[0]
    for e in range(1, owners):
        total = total + part_in[e]
    total_ref[...] = total
    for t in range(tilts):
        powers = []
        for kind in range(2):
            row = tilts * n + kind * tilts + t
            powers.append(
                jnp.sum(total[row : row + 1], axis=1, keepdims=True) / (band * band) + 1e-06
            )
        scale = band * jnp.sqrt(powers[0] * powers[1])
        corr = total[t * n : (t + 1) * n] / scale
        peak_ref[t] = jnp.max(corr)
        corr_ref[t] = total_ref[pl.ds(t * n + me, 1), :] / scale

    for group in scatters:
        for k in range(1, n):
            on_owner(lax.rem(me + k, n), lambda: copy_of(*group, k).wait_send())

    def drain():
        for k in range(1, n):
            copy_of(part_out, part_in, part_send, part_recv, k).wait_send()

    on_owner(me, drain)


def exchange(n, length, win_cols, center, owner, partial, mine):
    tilts, count, _ = partial.shape
    band = mine.shape[-1]
    per = max(1, band // 2 // n)
    owners = band // 2 // per
    message = tilts * n + 8 * pl.cdiv(2 * tilts, 8)
    smem = pl.BlockSpec(memory_space=pltpu.SMEM)
    vmem = pl.BlockSpec(memory_space=pltpu.VMEM)
    return pl.pallas_call(
        functools.partial(exchange_kernel, n, length),
        out_shape=(
            jax.ShapeDtypeStruct((tilts, 1, win_cols), F32),
            jax.ShapeDtypeStruct((tilts,), F32),
        ),
        in_specs=[smem, smem, vmem, vmem, vmem],
        out_specs=(vmem, smem),
        scratch_shapes=[
            pltpu.VMEM((owners, 4 * per, band), F32),
            pltpu.VMEM((n, 4 * per, band), F32),
            pltpu.VMEM((owners, tilts * 4 * per, band), F32),
            pltpu.VMEM((n, tilts * 4 * per, band), F32),
            pltpu.VMEM((message, win_cols), F32),
            pltpu.VMEM((n, message, win_cols), F32),
            pltpu.VMEM((message, win_cols), F32),
        ]
        + [pltpu.SemaphoreType.DMA((n,))] * 6,
        compiler_params=pltpu.CompilerParams(
            collective_id=0, has_side_effects=True, vmem_limit_bytes=56 * 1024 * 1024
        ),
        name="exchange",
    )(center, owner, partial, mine, jnp.asarray(window_table(length, band, win_cols)))


def solution(mesh):
    n = mesh.shape["slab"]

    def per_device(volume, shift, weight, left, share, center, owner, bands):
        band = bands.shape[-1]
        partial = partial_spectra(shift, weight, left, share, volume, band)
        return exchange(n, volume.shape[-1], band, center, owner, partial, bands)

    placed = (
        P(("grp", "slab"), None, None),
        P("grp", "slab"),
        P("grp", "slab"),
        P("grp", None),
        P("grp", None),
        P("grp", None),
        P("grp"),
        P(("grp", "slab"), None, None, None),
    )
    return jax.shard_map(
        per_device,
        mesh=mesh,
        in_specs=placed,
        out_specs=(P("grp", "slab", None), P("grp")),
        check_vma=False,
    )
```

time: 317 us -> 41.3 us (0.13)
  the two profiles are of different devices: /device:TPU:0 before, /device:TPU:9 now
where the time goes in v1:
time: 41.3 us; the launch traced here: 41.1 us
  Pallas kernels  38 us (92%)
  local copies, waits for them, and re-layouts  2.42 us (6%)
  between operations  0.65 us (2%)
    pallas_call x1, Pallas kernels, exchange(): pl.pallas_call(functools.partial(exchange_kernel, n, length), out_shape=(...  26.6 us
    pallas_call x1, Pallas kernels, partial_spectra(): pl.pallas_call(partial_kernel, out_shape=jax.ShapeDtypeStruct((tilts, cou...  11.5 us
    unnamed x2, local copies, waits for them, and re-layouts  2.42 us

profile of v1, /device:TPU:9, one launch (start us, length us, event | category | flops | bytes accessed | tf_op | source)
XLA Modules:
  0.0 41.1 jit_solution(7431098611653265122)
XLA Ops:
  0.6 11.5 %partial_spectra.1.partial_ref = f32[2,144,256]{2,1,0:T(8,128)} custom-call(s32[2,2]{1,0:T(2,128)} %shift_ref.1, f32[2,2]{1,0:T(2,128)} %weight_ref.1, s32[2,1024]{1,0:T(2,128)} %left_ref.1, f32[2,1024]{1,0:T(2,128)} %share_ref.1, bf16[2,1024,1024]{2,1,0:T(8,128)(2,1)} %volume_ref.1, bf16[288,1024]{1,0:T(8,128)(2,1)} %constant.6.clone.rowt_ref, ...), custom_call_target="tpu_custom_call" | custom-call | tf_op jit(solution)/shard_map/partial_spectra/pallas_call | solution.py:155
  12.1 26.6 %exchange.1 = (f32[2,1,128]{2,1,0:T(1,128)}, f32[2]{0:T(128)}) custom-call(s32[2,2]{1,0:T(2,128)} %center_ref.1, s32[16]{0:T(128)} %owner_ref.1, f32[2,144,256]{2,1,0:T(8,128)} %partial_spectra.1.partial_ref, f32[1,2,128,128]{3,2,1,0:T(8,128)} %mine_ref.1, f32[128,256]{1,0:T(8,128)} %constant.8.clone.window_ref), custom_call_target="tpu_custom_call" | custom-call | tf_op jit(solution)/shard_map/exchange/pallas_call | solution.py:359
  38.7 1.2 %copy.15 = f32[2,1,128]{2,1,0:T(1,128)} copy(f32[2,1,128]{2,1,0:T(1,128)} %get-tuple-element.4) | data formatting | bytes 2048
  39.9 1.2 %copy.16 = f32[2]{0:T(128)} copy(f32[2]{0:T(128)} %get-tuple-element.5) | data formatting | bytes 16

commit v2 on v1

v2 whole, which is shorter than its diff:
```python
import functools
import math

import jax
import jax.numpy as jnp
import numpy as np
from jax import lax
from jax.experimental import pallas as pl
from jax.experimental.pallas import tpu as pltpu
from jax.sharding import PartitionSpec as P

MESH = pl.DeviceIdType.MESH
LANES = 128
CHUNK = 256
BF16 = jnp.bfloat16
F32 = jnp.float32


def phases(left, right, length):
    angle = (np.outer(left, right) % length) * (2.0 * math.pi / length)
    return np.cos(angle), np.sin(angle)


def split(values):
    high = values.astype(np.float32).astype(BF16)
    low = (values - high.astype(np.float64)).astype(np.float32).astype(BF16)
    return high, low


def halves(value):
    high = value.astype(BF16)
    return high, (value - high.astype(F32)).astype(BF16)


def row_table(length, band):
    count = band // 2 + 8
    cos, sin = phases(np.arange(count), np.arange(length), length)
    return np.concatenate(split(np.concatenate([cos, sin])))


def col_table(length, band):
    cos, sin = phases(np.arange(length), np.arange(band), length)
    return np.stack(split(np.concatenate([cos, sin], axis=1)))


def window_table(length, band, columns):
    cos, sin = phases(np.arange(band), np.arange(columns), length)
    return np.concatenate([cos, sin], axis=1).astype(np.float32)


def fused_kernel(
    n, center_ref, owner_ref, shift_ref, weight_ref, left_ref, share_ref, mine_ref, window_ref,
    volume_ref, rowt_ref, colt_ref, out_ref,
    vol, rowt, colt, onehot, rows, rolled, summed, stack, proj, sems,
    ref_out, ref_in, spec_out, spec_in, part_out, part_in, peak_out, peak_in,
    ref_send, ref_recv, spec_send, spec_recv, part_send, part_recv, peak_send, peak_recv,
):
    me = lax.axis_index("slab")
    planes, height, width = volume_ref.shape
    tilts = left_ref.shape[0]
    blocks = width // LANES
    chunks = width // CHUNK
    count = rows.shape[2]

    table = pltpu.make_async_copy(rowt_ref, rowt, sems.at[0])
    table.start()
    loads = []
    for z in range(planes):
        for c in range(chunks):
            part = (z, slice(None), pl.ds(c * CHUNK, CHUNK))
            load = pltpu.make_async_copy(volume_ref.at[part], vol.at[part], sems.at[2 + z * chunks + c])
            load.start()
            loads.append(load)
    last_table = pltpu.make_async_copy(colt_ref, colt, sems.at[1])
    last_table.start()

    band = mine_ref.shape[-1]
    length = width
    half = band // 2
    sines = count // 2
    per = max(1, half // n)
    owners = half // per
    win_cols = out_ref.shape[-1]

    def on_owner(device, body):
        if owners == n:
            body()
        else:
            pl.when(device < owners)(body)

    barrier = pltpu.get_barrier_semaphore()
    for k in range(1, n):
        pl.semaphore_signal(
            barrier, inc=1, device_id={"slab": lax.rem(me + k, n)}, device_id_type=MESH
        )

    def sending(source, into, send, recv, k):
        return pltpu.make_async_remote_copy(
            src_ref=source,
            dst_ref=into.at[me],
            send_sem=send.at[k],
            recv_sem=recv.at[k],
            device_id={"slab": lax.rem(me + k, n)},
            device_id_type=MESH,
        )

    def arriving(into, send, recv, k):
        source = lax.rem(me + n - k, n)
        return pltpu.make_async_remote_copy(
            src_ref=into.at[source],
            dst_ref=into.at[source],
            send_sem=send.at[k],
            recv_sem=recv.at[k],
            device_id={"slab": source},
            device_id_type=MESH,
        )

    def scatter(out, into, send, recv, k):
        return sending(out.at[lax.rem(me + k, n)], into, send, recv, k)

    def scatter_all(*group):
        for k in range(1, n):
            on_owner(lax.rem(me + k, n), lambda: scatter(*group, k).start())

    refs = (ref_out, ref_in, ref_send, ref_recv)
    spectra = [
        (spec_out.at[t], spec_in.at[t], spec_send.at[t], spec_recv.at[t]) for t in range(tilts)
    ]

    for e in range(owners):
        for part in range(2):
            base = part * 2 * per
            first = half + e * per
            ref_out[e, base : base + per, :] = mine_ref[0, part, first : first + per, :]
            for k in range(per):
                row = (half - e * per - k) if e * per + k else 0
                ref_out[e, base + per + k : base + per + k + 1, :] = mine_ref[0, part, row : row + 1, :]

    @pl.loop(0, blocks)
    def _(b):
        first = pl.multiple_of(b * LANES, LANES)
        ids = lax.broadcasted_iota(jnp.int32, (LANES, width), 0) + first
        for t in range(tilts):
            hit = jnp.where(ids == left_ref[t : t + 1, :], 1.0, 0.0)
            onehot[t, pl.ds(first, LANES), :] = hit.astype(BF16)

    table.wait()
    for z in range(planes):
        for c in range(chunks):
            loads[z * chunks + c].wait()
            out = jnp.dot(
                rowt[...], vol[z, :, c * CHUNK : (c + 1) * CHUNK], preferred_element_type=F32
            )
            out = out[:count] + out[count:]
            for b in range(CHUNK // LANES):
                rows[z, c * (CHUNK // LANES) + b] = out[:, b * LANES : (b + 1) * LANES]
        if z == 0:
            pl.semaphore_wait(barrier, n - 1)
            scatter_all(*refs)

    lane = lax.broadcasted_iota(jnp.int32, (count, LANES), 1)
    zero = jnp.zeros((count, LANES), F32)
    top = lax.broadcasted_iota(jnp.int32, (half, band), 0) == 0
    for t in range(tilts):
        terms = []
        for z in range(planes):
            for extra in range(2):
                slot = z * 2 + extra
                shift = shift_ref[t, z] + extra
                turn = shift & (LANES - 1)
                jump = jnp.where(shift < 0, 1, 0)
                weight = weight_ref[t, z] if extra else 1.0 - weight_ref[t, z]
                rolled[slot, 0] = zero
                rolled[slot, blocks + 1] = zero
                for b in range(blocks):
                    rolled[slot, b + 1] = pltpu.roll(rows[z, b] * weight, turn, 1)
                terms.append((slot, lane >= turn, jump))
        for b in range(blocks):
            total = None
            for slot, mask, jump in terms:
                term = jnp.where(mask, rolled[slot, b + 1 + jump], rolled[slot, b + jump])
                total = term if total is None else total + term
            summed[b] = total
            high, low = halves(total)
            here = slice(b * LANES, (b + 1) * LANES)
            stack[0, :, here] = high
            stack[1, :, here] = low
        for b in range(blocks):
            ahead = summed[(b + 1) % blocks]
            right = pltpu.roll(jnp.where(lane == 0, ahead, summed[b]), LANES - 1, 1)
            high, low = halves(right)
            here = slice(b * LANES, (b + 1) * LANES)
            stack[2, :, here] = high
            stack[3, :, here] = low
        for c in range(chunks):
            here = slice(c * CHUNK, (c + 1) * CHUNK)
            picked = jnp.dot(
                stack[...].reshape(4 * count, width), onehot[t, :, here], preferred_element_type=F32
            )
            share = share_ref[t : t + 1, here]
            value = (1.0 - share) * (picked[:count] + picked[count : 2 * count])
            value = value + share * (picked[2 * count : 3 * count] + picked[3 * count :])
            high, low = halves(value)
            proj[0, :, here] = high
            proj[1, :, here] = low
        if t == 0:
            last_table.wait()
        both = jnp.dot(
            proj[...].reshape(2 * count, width), colt[0], preferred_element_type=F32
        )
        rest = jnp.dot(proj[0], colt[1], preferred_element_type=F32)
        partial = both[:count] + both[count:] + rest
        cos_cos = partial[:sines, :band]
        cos_sin = partial[:sines, band:]
        sin_cos = partial[sines:, :band]
        sin_sin = partial[sines:, band:]
        low_re = cos_cos + sin_sin
        low_im = sin_cos - cos_sin
        kinds = (
            (cos_cos - sin_sin)[:half],
            jnp.where(top, low_re[half : half + 1], low_re[:half]),
            -(sin_cos + cos_sin)[:half],
            jnp.where(top, low_im[half : half + 1], low_im[:half]),
        )
        for kind, value in enumerate(kinds):
            base = kind * per
            for e in range(owners):
                spec_out[t, e, base : base + per, :] = value[e * per : (e + 1) * per]
        scatter_all(*spectra[t])

    def wave(ints):
        angle = (ints & (length - 1)).astype(F32) * (2.0 * math.pi / length)
        return jnp.cos(angle), jnp.sin(angle)

    freq = lax.broadcasted_iota(jnp.int32, (2 * per, band), 1)
    slot = lax.broadcasted_iota(jnp.int32, (n, 2 * per), 1)
    step = lax.broadcasted_iota(jnp.int32, (n, 2 * per), 0) - n // 2
    lower = slot >= per
    place = me * per + jnp.where(lower, slot - per, slot)
    freq_row = jnp.where(lower, jnp.where(place == 0, -half, -place), place)
    col_waves = [wave(freq * (center_ref[t, 1] - win_cols // 2)) for t in range(tilts)]
    row_waves = [wave(freq_row * (center_ref[t, 0] + step)) for t in range(tilts)]
    spot = lax.broadcasted_iota(jnp.int32, (1, win_cols), 1)

    def contribute():
        ref_in[me] = ref_out[me]
        for k in range(1, n):
            arriving(*refs[1:], k).wait_recv()
        real_parts, imag_parts = [], []
        energy = jnp.zeros((1, win_cols), F32)
        for t in range(tilts):
            spec_in[t, me] = spec_out[t, me]
            for k in range(1, n):
                arriving(*spectra[t][1:], k).wait_recv()
            total = spec_in[t, 0]
            for e in range(1, n):
                total = total + spec_in[t, e]
            spec_re, spec_im = total[: 2 * per], total[2 * per :]
            owned = ref_in[owner_ref[t]]
            ref_re, ref_im = owned[: 2 * per], owned[2 * per :]
            cross_re = spec_re * ref_re + spec_im * ref_im
            cross_im = spec_im * ref_re - spec_re * ref_im
            cos, sin = col_waves[t]
            real_parts.append(cross_re * cos - cross_im * sin)
            imag_parts.append(cross_re * sin + cross_im * cos)
            for kind, (real, imag) in enumerate(((spec_re, spec_im), (ref_re, ref_im))):
                power = jnp.sum(real * real + imag * imag, axis=0, keepdims=True)
                power = jnp.sum(power, axis=1, keepdims=True)
                energy = jnp.where(spot == kind * tilts + t, power, energy)
        turned = jnp.dot(
            jnp.concatenate(real_parts + imag_parts, axis=0), window_ref[...],
            precision=lax.Precision.HIGHEST, preferred_element_type=F32,
        )
        mid = tilts * 2 * per
        moved_re = turned[:mid, :win_cols] - turned[mid:, win_cols:]
        moved_im = turned[:mid, win_cols:] + turned[mid:, :win_cols]
        for t in range(tilts):
            here = slice(t * 2 * per, (t + 1) * 2 * per)
            cos, sin = row_waves[t]
            left = jnp.concatenate([cos, -sin], axis=1)
            right = jnp.concatenate([moved_re[here], moved_im[here]], axis=0)
            value = jnp.dot(
                left, right, precision=lax.Precision.HIGHEST, preferred_element_type=F32
            )
            for i in range(n):
                part_out[i, t : t + 1, :] = value[i : i + 1]
        for i in range(n):
            part_out[i, tilts : tilts + 1, :] = energy
        for k in range(1, n):
            scatter(part_out, part_in, part_send, part_recv, k).start()
        part_in[me] = part_out[me]

    on_owner(me, contribute)

    for k in range(1, n):
        source = lax.rem(me + n - k, n)
        on_owner(source, lambda: arriving(part_in, part_send, part_recv, k).wait_recv())
    total = part_in[0]
    for e in range(1, owners):
        total = total + part_in[e]
    means = total[tilts : tilts + 1] / (band * band) + 1e-06
    lines = []
    for t in range(tilts):
        scale = band * jnp.sqrt(means[:, t : t + 1] * means[:, tilts + t : tilts + t + 1])
        lines.append(total[t : t + 1] / scale)
    line = jnp.concatenate(lines, axis=0)
    peak_out[...] = line
    for k in range(1, n):
        sending(peak_out, peak_in, peak_send, peak_recv, k).start()
    peak_in[me] = line
    out_ref[0] = line
    for group in [refs] + spectra:
        for k in range(1, n):
            on_owner(lax.rem(me + k, n), lambda: scatter(*group, k).wait_send())

    def drain():
        for k in range(1, n):
            scatter(part_out, part_in, part_send, part_recv, k).wait_send()

    on_owner(me, drain)
    for k in range(1, n):
        arriving(peak_in, peak_send, peak_recv, k).wait_recv()
    best = peak_in[0]
    for e in range(1, n):
        best = jnp.maximum(best, peak_in[e])
    out_ref[1] = best
    for k in range(1, n):
        sending(peak_out, peak_in, peak_send, peak_recv, k).wait_send()


def finish_kernel(both_ref, corr_ref, peak_ref):
    for t in range(both_ref.shape[1]):
        corr_ref[t] = both_ref[0, t : t + 1, :]
        peak_ref[t] = jnp.max(both_ref[1, t : t + 1, :])


def run(n, volume, shift, weight, left, share, center, owner, mine):
    planes, height, width = volume.shape
    tilts = left.shape[0]
    band = mine.shape[-1]
    win_cols = band
    rowt = row_table(height, band)
    colt = col_table(width, band)
    window = window_table(width, band, win_cols)
    count = rowt.shape[0] // 2
    blocks = width // LANES
    per = max(1, band // 2 // n)
    owners = band // 2 // per
    smem = pl.BlockSpec(memory_space=pltpu.SMEM)
    vmem = pl.BlockSpec(memory_space=pltpu.VMEM)
    hbm = pl.BlockSpec(memory_space=pl.ANY)
    dma = pltpu.SemaphoreType.DMA
    both = pl.pallas_call(
        functools.partial(fused_kernel, n),
        out_shape=jax.ShapeDtypeStruct((2, tilts, win_cols), F32),
        in_specs=[smem] * 4 + [vmem] * 4 + [hbm] * 3,
        out_specs=vmem,
        scratch_shapes=[
            pltpu.VMEM((planes, height, width), BF16),
            pltpu.VMEM(rowt.shape, BF16),
            pltpu.VMEM(colt.shape, BF16),
            pltpu.VMEM((tilts, width, width), BF16),
            pltpu.VMEM((planes, blocks, count, LANES), F32),
            pltpu.VMEM((planes * 2, blocks + 2, count, LANES), F32),
            pltpu.VMEM((blocks, count, LANES), F32),
            pltpu.VMEM((4, count, width), BF16),
            pltpu.VMEM((2, count, width), BF16),
            dma((2 + planes * (width // CHUNK),)),
            pltpu.VMEM((owners, 4 * per, band), F32),
            pltpu.VMEM((n, 4 * per, band), F32),
            pltpu.VMEM((tilts, owners, 4 * per, band), F32),
            pltpu.VMEM((tilts, n, 4 * per, band), F32),
            pltpu.VMEM((n, tilts + 1, win_cols), F32),
            pltpu.VMEM((n, tilts + 1, win_cols), F32),
            pltpu.VMEM((tilts, win_cols), F32),
            pltpu.VMEM((n, tilts, win_cols), F32),
            dma((n,)), dma((n,)), dma((tilts, n)), dma((tilts, n)),
            dma((n,)), dma((n,)), dma((n,)), dma((n,)),
        ],
        compiler_params=pltpu.CompilerParams(
            collective_id=0, has_side_effects=True, vmem_limit_bytes=56 * 1024 * 1024
        ),
        name="fused",
    )(
        center, owner, shift, weight, left, share, mine, jnp.asarray(window),
        volume, jnp.asarray(rowt), jnp.asarray(colt),
    )
    return pl.pallas_call(
        finish_kernel,
        out_shape=(
            jax.ShapeDtypeStruct((tilts, 1, win_cols), F32),
            jax.ShapeDtypeStruct((tilts,), F32),
        ),
        in_specs=[vmem],
        out_specs=(vmem, smem),
        name="finish",
    )(both)


def solution(mesh):
    n = mesh.shape["slab"]

    def per_device(volume, shift, weight, left, share, center, owner, bands):
        return run(n, volume, shift, weight, left, share, center, owner, bands)

    placed = (
        P(("grp", "slab"), None, None),
        P("grp", "slab"),
        P("grp", "slab"),
        P("grp", None),
        P("grp", None),
        P("grp", None),
        P("grp"),
        P(("grp", "slab"), None, None, None),
    )
    return jax.shard_map(
        per_device,
        mesh=mesh,
        in_specs=placed,
        out_specs=(P("grp", "slab", None), P("grp")),
        check_vma=False,
    )
```

time: 41.3 us -> 32.2 us (0.78)
  the two profiles are of different devices: /device:TPU:9 before, /device:TPU:0 now
where the time goes in v2:
time: 32.2 us; the launch traced here: 32 us
  Pallas kernels  31.4 us (98%)
  between operations  0.64 us (2%)
    pallas_call x1, Pallas kernels, run(): pl.pallas_call(functools.partial(fused_kernel, n), out_shape=jax.ShapeDty...  30.1 us
    pallas_call x1, Pallas kernels, run(): pl.pallas_call(finish_kernel, out_shape=(jax.ShapeDtypeStruct((tilts, 1,...  1.32 us

profile of v2, /device:TPU:0, one launch (start us, length us, event | category | flops | bytes accessed | tf_op | source)
XLA Modules:
  0.0 32.0 jit_solution(7820746667278908658)
XLA Ops:
  0.6 30.1 %fused.1.both_ref = f32[2,2,128]{2,1,0:T(2,128)} custom-call(s32[2,2]{1,0:T(2,128)} %center_ref.1, s32[16]{0:T(128)} %owner_ref.1, s32[2,2]{1,0:T(2,128)} %shift_ref.1, f32[2,2]{1,0:T(2,128)} %weight_ref.1, s32[2,1024]{1,0:T(2,128)} %left_ref.1, f32[2,1024]{1,0:T(2,128)} %share_ref.1, f32[1,2,128,128]{3,2,1,0:T(8,128)} %mine_ref.1, ...), custom_call_target="tpu_custom_call" | custom-call | tf_op jit(solution)/shard_map/fused/pallas_call | solution.py:353
  30.7 1.3 %finish.1 = (f32[2,1,128]{2,1,0:T(1,128)}, f32[2]{0:T(128)}) custom-call(f32[2,2,128]{2,1,0:T(2,128)} %fused.1.both_ref), custom_call_target="tpu_custom_call" | custom-call | tf_op jit(solution)/shard_map/finish/pallas_call | solution.py:388

commit v3 on v2

--- a/solution.py
+++ b/solution.py
@@ -32,6 +32,13 @@
     return high, (value - high.astype(F32)).astype(BF16)
 
 
+def product(first, second):
+    count = first[0].shape[0]
+    both = jnp.dot(jnp.concatenate(first, axis=0), second[0], preferred_element_type=F32)
+    rest = jnp.dot(first[0], second[1], preferred_element_type=F32)
+    return both[:count] + both[count:] + rest
+
+
 def row_table(length, band):
     count = band // 2 + 8
     cos, sin = phases(np.arange(count), np.arange(length), length)
@@ -45,13 +52,13 @@
 
 def window_table(length, band, columns):
     cos, sin = phases(np.arange(band), np.arange(columns), length)
-    return np.concatenate([cos, sin], axis=1).astype(np.float32)
+    return np.stack(split(np.concatenate([cos, sin], axis=1)))
 
 
 def fused_kernel(
     n, center_ref, owner_ref, shift_ref, weight_ref, left_ref, share_ref, mine_ref, window_ref,
     volume_ref, rowt_ref, colt_ref, out_ref,
-    vol, rowt, colt, onehot, rows, rolled, summed, stack, proj, sems,
+    vol, rowt, colt, mine_vmem, window_vmem, onehot, rolled, summed, stack, proj, sems,
     ref_out, ref_in, spec_out, spec_in, part_out, part_in, peak_out, peak_in,
     ref_send, ref_recv, spec_send, spec_recv, part_send, part_recv, peak_send, peak_recv,
 ):
@@ -60,7 +67,7 @@
     tilts = left_ref.shape[0]
     blocks = width // LANES
     chunks = width // CHUNK
-    count = rows.shape[2]
+    count = rowt.shape[0] // 2
 
     table = pltpu.make_async_copy(rowt_ref, rowt, sems.at[0])
     table.start()
@@ -68,11 +75,15 @@
     for z in range(planes):
         for c in range(chunks):
             part = (z, slice(None), pl.ds(c * CHUNK, CHUNK))
-            load = pltpu.make_async_copy(volume_ref.at[part], vol.at[part], sems.at[2 + z * chunks + c])
+            load = pltpu.make_async_copy(volume_ref.at[part], vol.at[part], sems.at[4 + z * chunks + c])
             load.start()
             loads.append(load)
     last_table = pltpu.make_async_copy(colt_ref, colt, sems.at[1])
     last_table.start()
+    mine_copy = pltpu.make_async_copy(mine_ref, mine_vmem, sems.at[2])
+    mine_copy.start()
+    window_copy = pltpu.make_async_copy(window_ref, window_vmem, sems.at[3])
+    window_copy.start()
 
     band = mine_ref.shape[-1]
     length = width
@@ -127,14 +138,15 @@
         (spec_out.at[t], spec_in.at[t], spec_send.at[t], spec_recv.at[t]) for t in range(tilts)
     ]
 
-    for e in range(owners):
-        for part in range(2):
-            base = part * 2 * per
-            first = half + e * per
-            ref_out[e, base : base + per, :] = mine_ref[0, part, first : first + per, :]
-            for k in range(per):
-                row = (half - e * per - k) if e * per + k else 0
-                ref_out[e, base + per + k : base + per + k + 1, :] = mine_ref[0, part, row : row + 1, :]
+    def order_refs():
+        for e in range(owners):
+            for part in range(2):
+                base = part * 2 * per
+                first = half + e * per
+                ref_out[e, base : base + per, :] = mine_vmem[0, part, first : first + per, :]
+                for k in range(per):
+                    row = (half - e * per - k) if e * per + k else 0
+                    ref_out[e, base + per + k : base + per + k + 1, :] = mine_vmem[0, part, row : row + 1, :]
 
     @pl.loop(0, blocks)
     def _(b):
@@ -143,6 +155,20 @@
         for t in range(tilts):
             hit = jnp.where(ids == left_ref[t : t + 1, :], 1.0, 0.0)
             onehot[t, pl.ds(first, LANES), :] = hit.astype(BF16)
+
+    lane = lax.broadcasted_iota(jnp.int32, (count, LANES), 1)
+    zero = jnp.zeros((count, LANES), F32)
+    top = lax.broadcasted_iota(jnp.int32, (half, band), 0) == 0
+    turns, jumps, weights = [], [], []
+    for t in range(tilts):
+        shifts = [shift_ref[t, z] for z in range(planes)]
+        turns.append([shift & (LANES - 1) for shift in shifts])
+        jumps.append([jnp.where(shift < 0, 1, 0) for shift in shifts])
+        weights.append([weight_ref[t, z] for z in range(planes)])
+        for z in range(planes):
+            rolled[t, z, 0] = zero
+            rolled[t, z, 1] = zero
+            rolled[t, z, blocks + 2] = zero
 
     table.wait()
     for z in range(planes):
@@ -153,62 +179,68 @@
             )
             out = out[:count] + out[count:]
             for b in range(CHUNK // LANES):
-                rows[z, c * (CHUNK // LANES) + b] = out[:, b * LANES : (b + 1) * LANES]
+                block = out[:, b * LANES : (b + 1) * LANES]
+                for t in range(tilts):
+                    rolled[t, z, c * (CHUNK // LANES) + b + 2] = pltpu.roll(block, turns[t][z], 1)
         if z == 0:
+            mine_copy.wait()
+            order_refs()
             pl.semaphore_wait(barrier, n - 1)
             scatter_all(*refs)
 
-    lane = lax.broadcasted_iota(jnp.int32, (count, LANES), 1)
-    zero = jnp.zeros((count, LANES), F32)
-    top = lax.broadcasted_iota(jnp.int32, (half, band), 0) == 0
+    def combine(t, b):
+        near, far = zero, zero
+        for z in range(planes):
+            jump = jumps[t][z]
+            if b < 0:
+                value = rolled[t, z, b + 2 + jump]
+            else:
+                value = jnp.where(
+                    lane >= turns[t][z], rolled[t, z, b + 2 + jump], rolled[t, z, b + 1 + jump]
+                )
+            near = near + (1.0 - weights[t][z]) * value
+            far = far + weights[t][z] * value
+        summed[t, 0, b + 1] = near
+        summed[t, 1, b + 1] = far
+
+    def place_block(t, b):
+        near, far = summed[t, 0, b + 1], summed[t, 1, b + 1]
+        ahead = summed[t, 0, (b + 1) % blocks + 1]
+        behind = summed[t, 1, b]
+        left = near + pltpu.roll(jnp.where(lane == LANES - 1, behind, far), 1, 1)
+        right = far + pltpu.roll(jnp.where(lane == 0, ahead, near), LANES - 1, 1)
+        here = slice(b * LANES, (b + 1) * LANES)
+        for slot, value in enumerate(halves(left) + halves(right)):
+            stack[t, slot, :, here] = value
+
+    def tasks(t):
+        made = [functools.partial(combine, t, b) for b in range(-1, blocks)]
+        return made + [functools.partial(place_block, t, b) for b in range(blocks)]
+
+    for task in tasks(0):
+        task()
     for t in range(tilts):
-        terms = []
-        for z in range(planes):
-            for extra in range(2):
-                slot = z * 2 + extra
-                shift = shift_ref[t, z] + extra
-                turn = shift & (LANES - 1)
-                jump = jnp.where(shift < 0, 1, 0)
-                weight = weight_ref[t, z] if extra else 1.0 - weight_ref[t, z]
-                rolled[slot, 0] = zero
-                rolled[slot, blocks + 1] = zero
-                for b in range(blocks):
-                    rolled[slot, b + 1] = pltpu.roll(rows[z, b] * weight, turn, 1)
-                terms.append((slot, lane >= turn, jump))
-        for b in range(blocks):
-            total = None
-            for slot, mask, jump in terms:
-                term = jnp.where(mask, rolled[slot, b + 1 + jump], rolled[slot, b + jump])
-                total = term if total is None else total + term
-            summed[b] = total
-            high, low = halves(total)
-            here = slice(b * LANES, (b + 1) * LANES)
-            stack[0, :, here] = high
-            stack[1, :, here] = low
-        for b in range(blocks):
-            ahead = summed[(b + 1) % blocks]
-            right = pltpu.roll(jnp.where(lane == 0, ahead, summed[b]), LANES - 1, 1)
-            high, low = halves(right)
-            here = slice(b * LANES, (b + 1) * LANES)
-            stack[2, :, here] = high
-            stack[3, :, here] = low
+        later = tasks(t + 1) if t + 1 < tilts else []
+        share_of = -(-len(later) // chunks)
         for c in range(chunks):
             here = slice(c * CHUNK, (c + 1) * CHUNK)
             picked = jnp.dot(
-                stack[...].reshape(4 * count, width), onehot[t, :, here], preferred_element_type=F32
+                stack[t].reshape(4 * count, width), onehot[t, :, here], preferred_element_type=F32
             )
             share = share_ref[t : t + 1, here]
             value = (1.0 - share) * (picked[:count] + picked[count : 2 * count])
             value = value + share * (picked[2 * count : 3 * count] + picked[3 * count :])
             high, low = halves(value)
-            proj[0, :, here] = high
-            proj[1, :, here] = low
+            proj[t, 0, :, here] = high
+            proj[t, 1, :, here] = low
+            for task in later[c * share_of : (c + 1) * share_of]:
+                task()
         if t == 0:
             last_table.wait()
         both = jnp.dot(
-            proj[...].reshape(2 * count, width), colt[0], preferred_element_type=F32
-        )
-        rest = jnp.dot(proj[0], colt[1], preferred_element_type=F32)
+            proj[t].reshape(2 * count, width), colt[0], preferred_element_type=F32
+        )
+        rest = jnp.dot(proj[t, 0], colt[1], preferred_element_type=F32)
         partial = both[:count] + both[count:] + rest
         cos_cos = partial[:sines, :band]
         cos_sin = partial[:sines, band:]
@@ -239,7 +271,11 @@
     place = me * per + jnp.where(lower, slot - per, slot)
     freq_row = jnp.where(lower, jnp.where(place == 0, -half, -place), place)
     col_waves = [wave(freq * (center_ref[t, 1] - win_cols // 2)) for t in range(tilts)]
-    row_waves = [wave(freq_row * (center_ref[t, 0] + step)) for t in range(tilts)]
+    row_waves = []
+    for t in range(tilts):
+        cos, sin = wave(freq_row * (center_ref[t, 0] + step))
+        row_waves.append(halves(jnp.concatenate([cos, -sin], axis=1)))
+    window_copy.wait()
     spot = lax.broadcasted_iota(jnp.int32, (1, win_cols), 1)
 
     def contribute():
@@ -267,21 +303,17 @@
                 power = jnp.sum(real * real + imag * imag, axis=0, keepdims=True)
                 power = jnp.sum(power, axis=1, keepdims=True)
                 energy = jnp.where(spot == kind * tilts + t, power, energy)
-        turned = jnp.dot(
-            jnp.concatenate(real_parts + imag_parts, axis=0), window_ref[...],
-            precision=lax.Precision.HIGHEST, preferred_element_type=F32,
+        turned = product(
+            halves(jnp.concatenate(real_parts + imag_parts, axis=0)),
+            (window_vmem[0], window_vmem[1]),
         )
         mid = tilts * 2 * per
         moved_re = turned[:mid, :win_cols] - turned[mid:, win_cols:]
         moved_im = turned[:mid, win_cols:] + turned[mid:, :win_cols]
         for t in range(tilts):
             here = slice(t * 2 * per, (t + 1) * 2 * per)
-            cos, sin = row_waves[t]
-            left = jnp.concatenate([cos, -sin], axis=1)
             right = jnp.concatenate([moved_re[here], moved_im[here]], axis=0)
-            value = jnp.dot(
-                left, right, precision=lax.Precision.HIGHEST, preferred_element_type=F32
-            )
+            value = product(row_waves[t], halves(right))
             for i in range(n):
                 part_out[i, t : t + 1, :] = value[i : i + 1]
         for i in range(n):
@@ -353,19 +385,20 @@
     both = pl.pallas_call(
         functools.partial(fused_kernel, n),
         out_shape=jax.ShapeDtypeStruct((2, tilts, win_cols), F32),
-        in_specs=[smem] * 4 + [vmem] * 4 + [hbm] * 3,
+        in_specs=[smem] * 4 + [vmem] * 2 + [hbm] * 5,
         out_specs=vmem,
         scratch_shapes=[
             pltpu.VMEM((planes, height, width), BF16),
             pltpu.VMEM(rowt.shape, BF16),
             pltpu.VMEM(colt.shape, BF16),
+            pltpu.VMEM(mine.shape, F32),
+            pltpu.VMEM(window.shape, BF16),
             pltpu.VMEM((tilts, width, width), BF16),
-            pltpu.VMEM((planes, blocks, count, LANES), F32),
-            pltpu.VMEM((planes * 2, blocks + 2, count, LANES), F32),
-            pltpu.VMEM((blocks, count, LANES), F32),
-            pltpu.VMEM((4, count, width), BF16),
-            pltpu.VMEM((2, count, width), BF16),
-            dma((2 + planes * (width // CHUNK),)),
+            pltpu.VMEM((tilts, planes, blocks + 3, count, LANES), F32),
+            pltpu.VMEM((tilts, 2, blocks + 1, count, LANES), F32),
+            pltpu.VMEM((tilts, 4, count, width), BF16),
+            pltpu.VMEM((tilts, 2, count, width), BF16),
+            dma((4 + planes * (width // CHUNK),)),
             pltpu.VMEM((owners, 4 * per, band), F32),
             pltpu.VMEM((n, 4 * per, band), F32),
             pltpu.VMEM((tilts, owners, 4 * per, band), F32),

time: 32.2 us -> 32.4 us (level)
  no operation moved by 1% of the time
where the time goes in v3:
time: 32.4 us; the launch traced here: 32.2 us
  Pallas kernels  31.6 us (98%)
  between operations  0.64 us (2%)
    pallas_call x1, Pallas kernels, run(): pl.pallas_call(functools.partial(fused_kernel, n), out_shape=jax.ShapeDty...  30.3 us
    pallas_call x1, Pallas kernels, run(): pl.pallas_call(finish_kernel, out_shape=(jax.ShapeDtypeStruct((tilts, 1,...  1.32 us

profile of v3, /device:TPU:0, one launch (start us, length us, event | category | flops | bytes accessed | tf_op | source)
XLA Modules:
  0.0 32.2 jit_solution(2732026306954319994)
XLA Ops:
  0.6 30.3 %fused.1.both_ref = f32[2,2,128]{2,1,0:T(2,128)} custom-call(s32[2,2]{1,0:T(2,128)} %center_ref.1, s32[16]{0:T(128)} %owner_ref.1, s32[2,2]{1,0:T(2,128)} %shift_ref.1, f32[2,2]{1,0:T(2,128)} %weight_ref.1, s32[2,1024]{1,0:T(2,128)} %left_ref.1, f32[2,1024]{1,0:T(2,128)} %share_ref.1, f32[1,2,128,128]{3,2,1,0:T(8,128)} %mine_ref.1, ...), custom_call_target="tpu_custom_call" | custom-call | tf_op jit(solution)/shard_map/fused/pallas_call | solution.py:385
  30.9 1.3 %finish.1 = (f32[2,1,128]{2,1,0:T(1,128)}, f32[2]{0:T(128)}) custom-call(f32[2,2,128]{2,1,0:T(2,128)} %fused.1.both_ref), custom_call_target="tpu_custom_call" | custom-call | tf_op jit(solution)/shard_map/finish/pallas_call | solution.py:421
